TPU v7x, 128 devices: a whole 4x4x4 slice. The times are simulated.
128 devices in a mesh: branch: 2 (over core), seq: 32 (over z, y, x_lo), mp: 2 (over x_hi).
Axes of the slice: x: 4 (x_hi: 2, x_lo: 2; x = x_hi * 2 + x_lo), y: 4, z: 4, core: 2. Of those that a mesh axis runs over, the one named last changes fastest.
Arguments:
- tokens: bfloat16 [8192, 4096], P('seq', 'mp'), may hold values from -6 to 6
- light_in: bfloat16 [4096, 2048], P(None, ('branch', 'mp')), may hold values from -0.09375 to 0.09375
- light_out: bfloat16 [2048, 4096], P(('branch', 'mp')), may hold values from -0.1875 to 0.1875
- heavy_in: bfloat16 [4096, 16384], P(None, ('branch', 'seq', 'mp')), may hold values from -0.09375 to 0.09375
- heavy_out: bfloat16 [16384, 4096], P(('branch', 'seq', 'mp')), may hold values from -0.1875 to 0.1875
- route_index: int32 [32, 32], P('seq'), may hold values from 0 to 255, as said below
- route_count: int32 [32], P('seq'), may hold values from 1 to 32, as said below
- route_gate: float32 [32, 32], P('seq'), may hold values from 0.25 to 2
- cotangent: bfloat16 [8192, 4096], P('seq', 'mp'), may hold values from -6 to 6
Outputs:
- mixed: bfloat16 [8192, 4096], P('seq', ('branch', 'mp'))
- grad_heavy_in: bfloat16 [4096, 16384], P(None, ('branch', 'seq', 'mp'))
- grad_heavy_out: bfloat16 [16384, 4096], P(('branch', 'seq', 'mp'))
Inputs may be any that keep to these rules, and one draw needn't show every extreme that they name: `route_index`: each row holds 32 distinct positions of its shard. The first route_count[s] slots of shard s are live; some shard has all 32 slots live.
All inputs are finite; a program needn't handle non-finite values.
Results may differ from a plain program's by a relative error of at most 0.008.
Values may be sent and summed in bfloat16 or wider, within the bound.
No kernel may reach another device: no remote copies, remote signals or barrier semaphores. Data moves between devices by JAX's collectives and lax.ppermute only.
A program may use at most 128 MiB of HBM per device.

v0:
```python
import jax
import jax.numpy as jnp
from jax import lax
from jax.sharding import PartitionSpec as P

root_coef = 0.7978845608
cubic_coef = 0.044715


def in_order(pieces, dim):
    pieces = jnp.moveaxis(pieces, 0, dim)
    shape = pieces.shape
    return pieces.reshape(*shape[:dim], shape[dim] * shape[dim + 1], *shape[dim + 2 :])


def from_everyone(x, axis):
    size = lax.axis_size(axis)
    return lax.all_to_all(jnp.broadcast_to(x[None], (size, *x.shape)), axis, 0, 0, tiled=True)


def gather_directly(x, axis, dim):
    return in_order(from_everyone(x, axis), dim)


def in_blocks(x, dim, size):
    shape = x.shape
    pieces = x.reshape(*shape[:dim], size, shape[dim] // size, *shape[dim + 1 :])
    return jnp.moveaxis(pieces, dim, 0)


def summed_on_arrival(x, axis, dim):
    pieces = in_blocks(x, dim, lax.axis_size(axis))
    arrived = lax.all_to_all(pieces, axis, split_axis=0, concat_axis=0, tiled=True)
    return arrived.sum(axis=0)


def sent_together(arrays, axis, dim, along):
    widths = [a.shape[along] for a in arrays]
    both = jnp.concatenate(arrays, axis=along)
    result = gather_directly(both, axis, dim)
    return tuple(jnp.split(result, [sum(widths[:k]) for k in range(1, len(widths))], axis=along))


def side_by_side(arrays, axis, dim, along):
    both = jnp.concatenate(arrays, axis=along)
    result, at, outs = (lax.all_gather(both, axis, axis=dim, tiled=True), 0, [])
    for a in arrays:
        outs.append(lax.slice_in_dim(result, at, at + a.shape[along], axis=along))
        at += a.shape[along]
    return tuple(outs)


def gelu_tanh(values):
    inner = root_coef * (values + cubic_coef * values * values * values)
    return 0.5 * values * (1.0 + jnp.tanh(inner))


def gelu_slope(values):
    tangent = jnp.tanh(root_coef * (values + cubic_coef * values * values * values))
    return 0.5 * (1.0 + tangent) + 0.5 * values * (1.0 - tangent * tangent) * root_coef * (
        1.0 + 3.0 * cubic_coef * values * values
    )


def over_rows(left, right):
    return lax.dot_general(
        left, right, (((0,), (0,)), ((), ())), preferred_element_type=jnp.float32
    )


def over_cols(left, right):
    return lax.dot_general(
        left, right, (((1,), (1,)), ((), ())), preferred_element_type=jnp.float32
    )


def per_device(
    tokens,
    light_in,
    light_out,
    heavy_in,
    heavy_out,
    route_index,
    route_count,
    route_gate,
    cotangent,
):
    whole = gather_directly(tokens, "mp", 1)
    light_hidden = gelu_tanh(jnp.dot(whole, light_in, preferred_element_type=jnp.float32)).astype(
        jnp.bfloat16
    )
    light_terms = jnp.dot(light_hidden, light_out, preferred_element_type=jnp.float32)
    light_share = summed_on_arrival(light_terms, ("branch", "mp"), 1)
    positions = route_index[0]
    slot_count = route_index.shape[1]
    live_slots = jnp.arange(slot_count, dtype=jnp.int32) < route_count[0]
    row_scale = jnp.where(live_slots, route_gate[0], jnp.zeros_like(route_gate[0]))
    picked = jnp.take(tokens, positions, axis=0)
    back_rows = (
        jnp.take(cotangent, positions, axis=0).astype(jnp.float32) * row_scale[:, None]
    ).astype(jnp.bfloat16)
    picked, back_rows = sent_together((picked, back_rows), "mp", 1, 0)
    picked, back_rows = side_by_side((picked, back_rows), "seq", 0, 1)
    pre_act = jnp.dot(picked, heavy_in, preferred_element_type=jnp.float32)
    heavy_hidden = gelu_tanh(pre_act).astype(jnp.bfloat16)
    grad_out = over_rows(heavy_hidden, back_rows).astype(jnp.bfloat16)
    slope = (over_cols(back_rows, heavy_out) * gelu_slope(pre_act)).astype(jnp.bfloat16)
    grad_in = over_rows(picked, slope).astype(jnp.bfloat16)
    group_hidden = gather_directly(heavy_hidden, ("branch", "mp"), 1)
    group_weight = lax.all_to_all(
        heavy_out, ("branch", "mp"), split_axis=1, concat_axis=0, tiled=True
    )
    partial_terms = jnp.dot(group_hidden, group_weight, preferred_element_type=jnp.float32)
    homed = lax.psum_scatter(
        partial_terms.astype(jnp.bfloat16), "seq", scatter_dimension=0, tiled=True
    ).astype(jnp.float32)
    heavy_share = homed * row_scale[:, None]
    mixed = light_share.at[positions].add(heavy_share).astype(jnp.bfloat16)
    return (mixed, grad_in, grad_out)


def solution(mesh):
    in_specs = (
        P("seq", "mp"),
        P(None, ("branch", "mp")),
        P(("branch", "mp"), None),
        P(None, ("branch", "seq", "mp")),
        P(("branch", "seq", "mp"), None),
        P("seq", None),
        P("seq"),
        P("seq", None),
        P("seq", "mp"),
    )
    out_specs = (
        P("seq", ("branch", "mp")),
        P(None, ("branch", "seq", "mp")),
        P(("branch", "seq", "mp"), None),
    )
    return jax.shard_map(
        per_device, mesh=mesh, in_specs=in_specs, out_specs=out_specs, check_vma=False
    )
```

profile of v0, /device:TPU:0, one launch (start us, length us, event | category | flops | bytes accessed | tf_op | source)
XLA Modules:
  0.0 641.6 jit_solution(16404235245912881351)
XLA Ops:
  9.3 2.1 gather_fusion.1
  11.4 2.1 gather_fusion
  14.5 13.7 %all_to_all.36 = bf16[2,64,2048]{2,1,0:T(8,128)(2,1)S(1)} all-to-all(bf16[2,64,2048]{2,1,0:T(8,128)(2,1)S(1)} %broadcast_in_dim.19), channel_id=1, replica_groups=mesh['branch'=2,'seq'=32,'mp'=2] {'mp'}, dimensions={0} | all-to-all | bytes 1048576 | tf_op jit(solution)/shard_map/all_to_all | solution.py:18
  29.1 1.6 copy.19
  30.8 1.3 copy.20
  32.1 4.3 all-to-all-start.4
  36.9 26.8 %all-to-all-done.4 = bf16[128,4,1024]{2,0,1:T(8,128)(2,1)} async-done(((bf16[128,4,1024]{2,0,1:T(8,128)(2,1)}), bf16[128,4,1024]{2,0,1:T(8,128)(2,1)}, u32[]{:S(2)}, u32[]{:S(2)}) %all-to-all-start.4) | async-done | bytes 1048608 | tf_op jit(solution)/shard_map/all_to_all | solution.py:110
  63.7 1.5 broadcast_in_dim.17
  65.1 3.8 all-to-all-start
  68.9 357.6 %all-gather.2.cloned.1.call-done = bf16[1024,8192]{1,0:T(8,128)(2,1)} async-done(((bf16[32,8192]{1,0:T(8,128)(2,1)}), bf16[1024,8192]{1,0:T(8,128)(2,1)}) %all-gather.2.cloned.1.call-update) | async-done | bytes 16777232 | tf_op jit(solution)/shard_map/all_gather | solution.py:46
  426.5 6.5 %multiply_convert_fusion = (bf16[1024,128]{1,0:T(8,128)(2,1)S(1)}, f32[1024,128]{1,0:T(8,128)}) fusion(bf16[4096,128]{1,0:T(8,128)(2,1)S(1)} %copy-done, bf16[1024,8192]{1,0:T(8,128)(2,1)} %all-gather.2.cloned.1.call-done), kind=kOutput, calls=%fused_computation.33 | convolution fusion | flops 1074921472 | bytes 10223616 | tf_op jit(solution)/shard_map/dot_general | solution.py:104
  433.0 1.1 broadcast_in_dim.20
  434.1 4.3 all-to-all-start.3
  438.4 8.0 %fusion.34 = f32[256,4096]{1,0:T(8,128)} fusion(bf16[512,4096]{1,0:T(8,128)(2,1)} %param.13, bf16[256,4096]{0,1:T(8,128)(2,1)S(1)} %bitcast.46, bf16[4096,512]{1,0:T(8,128)(2,1)} %param.12), kind=kOutput, calls=%fused_computation.34 | convolution fusion | flops 2148663296 | bytes 14680064 | tf_op jit(solution)/shard_map/dot_general | solution.py:92
  446.3 4.7 copy.25
  451.1 3.3 all-to-all-done.3
  454.4 4.8 all-to-all-start.1
  459.5 4.2 bitcast_convert_fusion
  463.7 59.1 %all-to-all-done.1 = f32[4,256,1024]{2,1,0:T(8,128)} async-done(((f32[4,256,1024]{2,1,0:T(8,128)}), f32[4,256,1024]{2,1,0:T(8,128)}, u32[]{:S(2)}, u32[]{:S(2)}) %all-to-all-start.1) | async-done | bytes 4194336 | tf_op jit(solution)/shard_map/all_to_all | solution.py:33
  522.8 2.7 reduce_sum.9
  525.5 5.7 fusion.11
  531.3 15.6 %fusion.8 = bf16[4096,128]{1,0:T(8,128)(2,1)} fusion(bf16[1024,8192]{1,0:T(8,128)(2,1)} %all-gather.2.cloned.1.call-done, bf16[128,4096]{1,0:T(8,128)(2,1)S(1)} %copy-done.2, f32[1024,128]{1,0:T(8,128)} %get-tuple-element.7), kind=kOutput, calls=%fused_computation.11 | convolution fusion | flops 2150498304 | bytes 19398656 | tf_op jit(solution)/shard_map/dot_general | solution.py:66
  546.9 85.4 %reduce-scatter.2.cloned.1.call-done = bf16[32,1024]{1,0:T(8,128)(2,1)} async-done(((bf16[1024,1024]{1,0:T(8,128)(2,1)}), bf16[32,1024]{1,0:T(8,128)(2,1)}) %reduce-scatter.2.cloned.1.call-update) | async-done | bytes 65552 | tf_op jit(solution)/shard_map/reduce_scatter | solution.py:114
  632.3 1.6 scatter_custom_fusion
  (28 shorter events, 4.9 us)
Async XLA Ops:
  7.2 419.3 %copy-start = (bf16[4096,128]{1,0:T(8,128)(2,1)S(1)}, bf16[4096,128]{1,0:T(8,128)(2,1)}, u32[]{:S(2)}) copy-start(bf16[4096,128]{1,0:T(8,128)(2,1)} %param.14) | copy-start | bytes 3145732
  7.2 419.3 %all-gather.2.cloned.1.call-start = ((), (), s32[]{:S(2)}) async-start(), calls=%async_computation.6 | async-start | bytes 17301504 | tf_op jit(solution)/shard_map/all_gather | solution.py:46
  28.2 8.1 %copy-start.1 = (bf16[256,2048]{1,0:T(8,128)(2,1)S(1)}, bf16[256,2048]{1,0:T(8,128)(2,1)}, u32[]{:S(2)}) copy-start(bf16[256,2048]{1,0:T(8,128)(2,1)} %param.11) | copy-start | bytes 3145732
  32.1 31.6 %all-to-all-start.4 = ((bf16[128,4,1024]{2,0,1:T(8,128)(2,1)}), bf16[128,4,1024]{2,0,1:T(8,128)(2,1)}, u32[]{:S(2)}, u32[]{:S(2)}) async-start(bf16[128,4,1024]{2,0,1:T(8,128)(2,1)} %copy.20), calls=%async_computation.4 | async-start | bytes 2097152 | tf_op jit(solution)/shard_map/all_to_all | solution.py:110
  65.1 367.9 %all-to-all-start = ((bf16[2,256,2048]{1,2,0:T(8,128)(2,1)}), bf16[2,256,2048]{1,2,0:T(8,128)(2,1)S(1)}, u32[]{:S(2)}, u32[]{:S(2)}) async-start(bf16[2,256,2048]{1,2,0:T(8,128)(2,1)} %broadcast_in_dim.17), calls=%async_computation | async-start | bytes 4194304 | tf_op jit(solution)/shard_map/all_to_all | solution.py:18
  434.1 20.3 %all-to-all-start.3 = ((bf16[4,1024,128]{2,1,0:T(8,128)(2,1)}), bf16[4,1024,128]{2,1,0:T(8,128)(2,1)}, u32[]{:S(2)}, u32[]{:S(2)}) async-start(bf16[4,1024,128]{2,1,0:T(8,128)(2,1)} %broadcast_in_dim.20), calls=%async_computation.3 | async-start | bytes 2097152 | tf_op jit(solution)/shard_map/all_to_all | solution.py:18
  454.4 68.4 %all-to-all-start.1 = ((f32[4,256,1024]{2,1,0:T(8,128)}), f32[4,256,1024]{2,1,0:T(8,128)}, u32[]{:S(2)}, u32[]{:S(2)}) async-start(f32[4,256,1024]{2,1,0:T(8,128)} %bitcast.45), calls=%async_computation.1 | async-start | bytes 8388608 | tf_op jit(solution)/shard_map/all_to_all | solution.py:33
  459.2 4.4 copy-start.3
  459.2 173.1 %reduce-scatter.2.cloned.1.call-start = ((), (), s32[]{:S(2)}) async-start(), calls=%async_computation.7 | async-start | bytes 2162688 | tf_op jit(solution)/shard_map/reduce_scatter | solution.py:114
  525.5 5.7 copy-start.2
Sparse Core Ops, SparseCore 0:
  29.3 397.1 all-gather.1
  463.8 168.4 reduce-scatter.1
where the time goes:
time: 642 us
  waiting for transfers between devices  532 us (83%)
  matrix products  40 us (6%)
  starting transfers between devices  17.4 us (3%)
  local copies, waits for them, and re-layouts  15.2 us (2%)
  between operations  14.9 us (2%)
  blocking collectives  13.7 us (2%)
  other arithmetic  8.33 us (1%)
    all_gather x1, waiting for transfers between devices, side_by_side(): result, at, outs = (lax.all_gather(both, axis, axis=dim, tiled=True), 0, [])  358 us
    reduce_scatter x1, waiting for transfers between devices, per_device(): lax.psum_scatter(partial_terms.astype(jnp.bfloat16), 'seq', scatter_dimen...  85.4 us
    all_to_all x1, waiting for transfers between devices, summed_on_arrival(): lax.all_to_all(pieces, axis, split_axis=0, concat_axis=0, tiled=True)  59.1 us
    all_to_all x1, waiting for transfers between devices, per_device(): lax.all_to_all(heavy_out, ('branch', 'mp'), split_axis=1, concat_axis=0,...  26.8 us
    dot_general x2, matrix products, over_rows(): lax.dot_general(left, right, (((0,), (0,)), ((), ())), preferred_element_...  21.3 us
    all_to_all x1, blocking collectives, from_everyone(): lax.all_to_all(jnp.broadcast_to(x[None], (size, *x.shape)), axis, 0, 0, t...  13.7 us
  transfers between devices with their start and end apart: 6, of which 5 were waited for; matrix products, arithmetic and copies ran while one was open for 8% of the time, Pallas kernels for 0%

commit v1 on v0

v1 whole, which is shorter than its diff:
```python
import jax
import jax.numpy as jnp
from jax import lax
from jax.sharding import Mesh, PartitionSpec as P

root_coef = 0.7978845608
cubic_coef = 0.044715

swap = [(0, 1), (1, 0)]


def gelu_tanh(values):
    inner = root_coef * (values + cubic_coef * values * values * values)
    return 0.5 * values * (1.0 + jnp.tanh(inner))


def gelu_slope(values):
    tangent = jnp.tanh(root_coef * (values + cubic_coef * values * values * values))
    return 0.5 * (1.0 + tangent) + 0.5 * values * (1.0 - tangent * tangent) * root_coef * (
        1.0 + 3.0 * cubic_coef * values * values
    )


def dot(left, right):
    return jnp.dot(left, right, preferred_element_type=jnp.float32)


def general(left, right, left_dims, right_dims):
    return lax.dot_general(
        left, right, ((left_dims, right_dims), ((), ())), preferred_element_type=jnp.float32
    )


def part(x, index, size, dim):
    return lax.dynamic_slice_in_dim(x, index * size, size, axis=dim)


def ordered(first, mine, other, dim):
    return jnp.where(
        first, jnp.concatenate([mine, other], dim), jnp.concatenate([other, mine], dim)
    )


def per_device(
    tokens,
    light_in,
    light_out,
    heavy_in,
    heavy_out,
    route_index,
    route_count,
    route_gate,
    cotangent,
):
    core = lax.axis_index("b")
    side = lax.axis_index("xh")
    rows, width = tokens.shape
    slots = route_index.shape[1]
    half = slots // 2

    positions = route_index[0]
    live_slots = jnp.arange(slots, dtype=jnp.int32) < route_count[0]
    row_scale = jnp.where(live_slots, route_gate[0], jnp.zeros_like(route_gate[0]))
    own_positions = part(positions, core, half, 0)
    own_scale = part(row_scale, core, half, 0)
    picked = jnp.take(tokens, own_positions, axis=0, mode="clip")
    back = jnp.take(cotangent, own_positions, axis=0, mode="clip").astype(jnp.float32)
    back = (back * own_scale[:, None]).astype(jnp.bfloat16)
    routed = jnp.concatenate([picked, back], axis=1)
    routed = lax.all_gather(routed, ("xh", "xl", "y", "z", "b"), axis=0, tiled=True)
    routed = routed.reshape(2, routed.shape[0] // 2, 2 * width)

    block = heavy_out.shape[1] // 4
    pieces = []
    for core_off in (0, 1):
        for side_off in (0, 1):
            target = (core ^ core_off) * 2 + (side ^ side_off)
            piece = part(heavy_out, target, block, 1)
            if core_off or side_off:
                pairs = [(k, k ^ (core_off * 2 + side_off)) for k in range(4)]
                piece = lax.ppermute(piece, ("b", "xh"), pairs)
            pieces.append(piece)
    group_weight = jnp.concatenate(pieces, axis=0)

    sent = part(tokens, core, rows // 2, 0)
    got = lax.ppermute(sent, "xh", swap)
    other = ordered(core == 0, got, lax.ppermute(got, "b", swap), 0)
    whole = ordered(side == 0, tokens, other, 1)
    light_hidden = gelu_tanh(dot(whole, light_in)).astype(jnp.bfloat16)
    mine = dot(light_hidden, part(light_out, core, width, 1))
    theirs = dot(light_hidden, part(light_out, 1 - core, width, 1))
    chip_terms = mine + lax.ppermute(theirs, "b", swap)
    light_share = part(chip_terms, side, block, 1) + lax.ppermute(
        part(chip_terms, 1 - side, block, 1).astype(jnp.bfloat16), "xh", swap
    ).astype(jnp.float32)

    in_weight = heavy_in.reshape(2, width, heavy_in.shape[1])
    out_weight = heavy_out
    pre_act = dot(routed[0, :, :width], in_weight[0]) + dot(routed[1, :, :width], in_weight[1])
    heavy_hidden = gelu_tanh(pre_act).astype(jnp.bfloat16)
    across = lax.ppermute(heavy_hidden, "xh", swap)
    pair = jnp.concatenate([heavy_hidden, across], axis=1)
    group_hidden = jnp.concatenate([pair, lax.ppermute(pair, "b", swap)], axis=1)
    partial_terms = dot(group_hidden, group_weight).astype(jnp.bfloat16)
    arrived = lax.all_to_all(partial_terms, ("xl", "y", "z"), 0, 0, tiled=True)
    homed = arrived.reshape(-1, slots, block).astype(jnp.float32).sum(axis=0)
    heavy_share = homed * row_scale[:, None]
    mixed = light_share.at[positions].add(heavy_share).astype(jnp.bfloat16)

    grad_out = jnp.concatenate(
        [general(heavy_hidden, routed[k, :, width:], (0,), (0,)) for k in (0, 1)], axis=1
    ).astype(jnp.bfloat16)
    slope = general(routed[0, :, width:], out_weight[:, :width], (1,), (1,)) + general(
        routed[1, :, width:], out_weight[:, width:], (1,), (1,)
    )
    slope = (slope * gelu_slope(pre_act)).astype(jnp.bfloat16)
    grad_in = jnp.concatenate(
        [general(routed[k, :, :width], slope, (0,), (0,)) for k in (0, 1)], axis=0
    ).astype(jnp.bfloat16)
    return (mixed, grad_in, grad_out)


def solution(mesh):
    split = Mesh(mesh.devices.reshape(2, 4, 4, 2, 2), ("b", "z", "y", "xl", "xh"))
    seq = ("z", "y", "xl")
    units = ("b", "z", "y", "xl", "xh")
    in_specs = (
        P(seq, "xh"),
        P(None, ("b", "xh")),
        P(("b", "xh"), None),
        P(None, units),
        P(units, None),
        P(seq, None),
        P(seq),
        P(seq, None),
        P(seq, "xh"),
    )
    out_specs = (
        P(seq, ("b", "xh")),
        P(None, units),
        P(units, None),
    )
    return jax.shard_map(
        per_device, mesh=split, in_specs=in_specs, out_specs=out_specs, check_vma=False
    )
```

time: 642 us -> 190 us (0.30)
  waiting for transfers between devices: 532 us -> 98.3 us
  blocking collectives: 13.7 us -> 0 us
  local copies, waits for them, and re-layouts: 15.2 us -> 7.52 us
    all_gather x1, waiting for transfers between devices: 358 us -> 45.7 us  [per_device(): lax.all_gather(routed, ('xh', 'xl', 'y', 'z', 'b'), axis=0, tiled=True)]
    reduce_scatter x1 -> x0, waiting for transfers between devices: 85.4 us -> none  [per_device(): lax.psum_scatter(partial_terms.astype(jnp.bfloat16), 'seq', scatter_dimen...]
    all_to_all x4 -> x1, waiting for transfers between devices: 89.2 us -> 16.3 us  [per_device(): arrived = lax.all_to_all(partial_terms, ('xl', 'y', 'z'), 0, 0, tiled=True)]
    ppermute x0 -> x9, waiting for transfers between devices: none -> 36.3 us  [the longest x1 12.9 us: per_device(): lax.ppermute(part(chip_terms, 1 - side, block, 1).astype(jnp.bfloat16), '...]
    ppermute x0 -> x9, starting transfers between devices: none -> 14.1 us  [the longest x1 3.71 us: per_device(): lax.ppermute(part(chip_terms, 1 - side, block, 1).astype(jnp.bfloat16), '...]
    all_to_all x1 -> x0, blocking collectives: 13.7 us -> none  [from_everyone(): lax.all_to_all(jnp.broadcast_to(x[None], (size, *x.shape)), axis, 0, 0, t...]
    all_to_all x4 -> x1, starting transfers between devices: 17.1 us -> 6.93 us  [per_device(): arrived = lax.all_to_all(partial_terms, ('xl', 'y', 'z'), 0, 0, tiled=True)]
    dot_general x5 -> x12, matrix products: 40 us -> 35.3 us  [the longest x6 19.9 us: dot(): return jnp.dot(left, right, preferred_element_type=jnp.float32)]
  transfers between devices with their start and end apart: 6 -> 11, of which waited for: 5 -> 7; matrix products, arithmetic and copies ran while one was open for 8% -> 21% of each run, Pallas kernels for 0% -> 0%
where the time goes in v1:
time: 190 us; the launch traced here: 189 us
  waiting for transfers between devices  98.3 us (52%)
  matrix products  35.3 us (19%)
  starting transfers between devices  21.1 us (11%)
  between operations  15 us (8%)
  other arithmetic  11.4 us (6%)
  local copies, waits for them, and re-layouts  7.52 us (4%)
    all_gather x1, waiting for transfers between devices, per_device(): lax.all_gather(routed, ('xh', 'xl', 'y', 'z', 'b'), axis=0, tiled=True)  45.7 us
    dot_general x6, matrix products, dot(): return jnp.dot(left, right, preferred_element_type=jnp.float32)  19.9 us
    all_to_all x1, waiting for transfers between devices, per_device(): arrived = lax.all_to_all(partial_terms, ('xl', 'y', 'z'), 0, 0, tiled=True)  16.3 us
    dot_general x6, matrix products, general(): lax.dot_general(left, right, ((left_dims, right_dims), ((), ())), preferr...  15.4 us
    ppermute x1, waiting for transfers between devices, per_device(): lax.ppermute(part(chip_terms, 1 - side, block, 1).astype(jnp.bfloat16), '...  12.9 us
    ppermute x1, waiting for transfers between devices, per_device(): got = lax.ppermute(sent, 'xh', swap)  11.9 us
    all_to_all x1, starting transfers between devices, per_device(): arrived = lax.all_to_all(partial_terms, ('xl', 'y', 'z'), 0, 0, tiled=True)  6.93 us
    ppermute x1, waiting for transfers between devices, per_device(): across = lax.ppermute(heavy_hidden, 'xh', swap)  5.46 us
  transfers between devices with their start and end apart: 11, of which 7 were waited for; matrix products, arithmetic and copies ran while one was open for 21% of the time, Pallas kernels for 0%

profile of v1, /device:TPU:0, one launch (start us, length us, event | category | flops | bytes accessed | tf_op | source)
XLA Modules:
  0.0 188.7 jit_solution(14561408914995607537)
XLA Ops:
  14.0 3.2 %collective-permute-start = (bf16[128,2048]{1,0:T(8,128)(2,1)S(1)}, bf16[128,2048]{1,0:T(8,128)(2,1)S(1)}, u32[]{:S(2)}, u32[]{:S(2)}) collective-permute-start(bf16[128,2048]{1,0:T(8,128)(2,1)S(1)} %constant_dynamic-slice_fusion.5), channel_id=1, source_target_pairs={{0,1},{1,0},{2,3},{3,2},{4,5},{5,4},{6,7},{7,6},{8,9},{9,8},{10,11... | collective-permute-start | bytes 1572872 | tf_op jit(solution)/shard_map/ppermute | solution.py:86
  17.2 11.9 %collective-permute-done = bf16[128,2048]{1,0:T(8,128)(2,1)S(1)} collective-permute-done((bf16[128,2048]{1,0:T(8,128)(2,1)S(1)}, bf16[128,2048]{1,0:T(8,128)(2,1)S(1)}, u32[]{:S(2)}, u32[]{:S(2)}) %collective-permute-start) | collective-permute-done | bytes 524320 | tf_op jit(solution)/shard_map/ppermute | solution.py:86
  31.3 3.8 %fusion.42 = bf16[256,512]{1,0:T(8,128)(2,1)S(1)} fusion(bf16[4096,512]{1,0:T(8,128)(2,1)} %param.10, bf16[256,2048]{1,0:T(8,128)(2,1)S(1)} %maximum_select_fusion.2, bf16[256,2048]{1,0:T(8,128)(2,1)S(1)} %copy-done.3, pred[]{:T(512)S(6)} %eq.6), kind=kOutput, calls=%fused_computation.61 | convolution fusion | flops 1084358656 | bytes 6553601 | tf_op jit(solution)/shard_map/dot_general | solution.py:25
  36.0 4.2 %collective-permute-done.2 = f32[256,2048]{1,0:T(8,128)} collective-permute-done((f32[256,2048]{1,0:T(8,128)S(1)}, f32[256,2048]{1,0:T(8,128)}, u32[]{:S(2)}, u32[]{:S(2)}) %collective-permute-start.2) | collective-permute-done | bytes 2097184 | tf_op jit(solution)/shard_map/ppermute | solution.py:92
  40.2 2.9 %convolution_add_fusion = f32[256,2048]{1,0:T(8,128)S(1)} fusion(f32[256,2048]{1,0:T(8,128)} %collective-permute-done.2, bf16[256,512]{1,0:T(8,128)(2,1)S(1)} %fusion.42, bf16[512,4096]{1,0:T(8,128)(2,1)} %param.11, s32[]{:T(128)S(6)} %select_n.70), kind=kOutput, calls=%fused_computation.16 | convolution fusion | flops 537395200 | bytes 6553604 | tf_op jit(solution)/shard_map/dot_general | solution.py:25
  44.0 3.7 %collective-permute-start.3 = (bf16[256,1024]{1,0:T(8,128)(2,1)}, bf16[256,1024]{1,0:T(8,128)(2,1)}, u32[]{:S(2)}, u32[]{:S(2)}) collective-permute-start(bf16[256,1024]{1,0:T(8,128)(2,1)} %dynamic-slice_convert_fusion), channel_id=1, source_target_pairs={{0,1},{1,0},{2,3},{3,2},{4,5},{5,4},{6,7},{7,6},{8,9},{9,8},{10,11... | collective-permute-start | bytes 1572872 | tf_op jit(solution)/shard_map/ppermute | solution.py:93
  47.7 2.1 %constant_dynamic-slice_fusion.3 = (bf16[128,1024]{1,0:T(8,128)(2,1)S(1)}, bf16[128,1024]{1,0:T(8,128)(2,1)}, bf16[128,1024]{1,0:T(8,128)(2,1)}, bf16[128,1024]{1,0:T(8,128)(2,1)}) fusion(bf16[128,4096]{1,0:T(8,128)(2,1)} %param.13, s32[]{:T(128)S(6)} %select_n.77, s32[]{:T(128)S(6)} %select_n.80, s32[]{:T(128)S(6)} %select_n.79, s32[]{:T(128)S(6)} %select_n.78), kind=kLoop, calls=%fused_computation.83 | loop fusion | bytes 2097168 | tf_op jit(solution)/shard_map/dynamic_slice | solution.py:35
  49.9 3.5 %collective-permute-start.6 = (bf16[128,1024]{1,0:T(8,128)(2,1)}, bf16[128,1024]{1,0:T(8,128)(2,1)}, u32[]{:S(2)}, u32[]{:S(2)}) collective-permute-start(bf16[128,1024]{1,0:T(8,128)(2,1)} %get-tuple-element.6), channel_id=1, source_target_pairs={{0,1},{1,0},{64,65},{65,64},{2,3},{3,2},{66,67},{67,66},{4,5},{5,4... | collective-permute-start | bytes 786440 | tf_op jit(solution)/shard_map/ppermute | solution.py:81
  53.5 12.9 %collective-permute-done.3 = bf16[256,1024]{1,0:T(8,128)(2,1)} collective-permute-done((bf16[256,1024]{1,0:T(8,128)(2,1)}, bf16[256,1024]{1,0:T(8,128)(2,1)}, u32[]{:S(2)}, u32[]{:S(2)}) %collective-permute-start.3) | collective-permute-done | bytes 524320 | tf_op jit(solution)/shard_map/ppermute | solution.py:93
  66.4 2.1 %convert_add_fusion = f32[256,1024]{1,0:T(8,128)} fusion(bf16[256,1024]{1,0:T(8,128)(2,1)} %collective-permute-done.3, f32[256,2048]{1,0:T(8,128)S(1)} %convolution_add_fusion, s32[]{:T(128)S(6)} %select_n.72), kind=kLoop, calls=%fused_computation.52 | loop fusion | flops 524288 | bytes 2621444 | tf_op jit(solution)/shard_map/add | solution.py:93
  68.5 45.7 %all-gather.2.cloned.1.call-done = bf16[2048,4096]{1,0:T(8,128)(2,1)} async-done(((bf16[16,4096]{1,0:T(8,128)(2,1)}), bf16[2048,4096]{1,0:T(8,128)(2,1)}) %all-gather.2.cloned.1.call-update) | async-done | bytes 16777232 | tf_op jit(solution)/shard_map/all_gather | solution.py:70
  114.2 4.0 %fusion.1 = f32[1024,128]{0,1:T(8,128)S(1)} fusion(bf16[2,1024,4096]{2,1,0:T(8,128)(2,1)} %bitcast.54, bf16[4096,128]{1,0:T(8,128)(2,1)} %param.12), kind=kOutput, calls=%fused_computation.9 | convolution fusion | flops 536870912 | bytes 5242880 | tf_op jit(solution)/shard_map/dot_general | solution.py:25
  118.2 4.7 %multiply_convert_fusion = (bf16[1024,128]{0,1:T(8,128)(2,1)S(1)}, f32[1024,128]{0,1:T(8,128)S(1)}) fusion(f32[1024,128]{0,1:T(8,128)S(1)} %fusion.1, bf16[4096,128]{1,0:T(8,128)(2,1)} %param.12, bf16[2,1024,4096]{2,1,0:T(8,128)(2,1)} %bitcast.55), kind=kOutput, calls=%fused_computation.70 | convolution fusion | flops 538181632 | bytes 6029312 | tf_op jit(solution)/shard_map/dot_general | solution.py:25
  122.9 3.1 %collective-permute-start.4 = (bf16[1024,128]{0,1:T(8,128)(2,1)S(1)}, bf16[1024,128]{0,1:T(8,128)(2,1)S(1)}, u32[]{:S(2)}, u32[]{:S(2)}) collective-permute-start(bf16[1024,128]{0,1:T(8,128)(2,1)S(1)} %get-tuple-element.7), channel_id=1, source_target_pairs={{0,1},{1,0},{2,3},{3,2},{4,5},{5,4},{6,7},{7,6},{8,9},{9,8},{10,11... | collective-permute-start | bytes 786440 | tf_op jit(solution)/shard_map/ppermute | solution.py:101
  127.5 5.5 %collective-permute-done.4 = bf16[1024,128]{0,1:T(8,128)(2,1)S(1)} collective-permute-done((bf16[1024,128]{0,1:T(8,128)(2,1)S(1)}, bf16[1024,128]{0,1:T(8,128)(2,1)S(1)}, u32[]{:S(2)}, u32[]{:S(2)}) %collective-permute-start.4) | collective-permute-done | bytes 262176 | tf_op jit(solution)/shard_map/ppermute | solution.py:101
  133.2 2.4 %fusion.25 = bf16[1024,128]{0,1:T(8,128)(2,1)} fusion(f32[1024,128]{0,1:T(8,128)S(1)} %fusion.5, bf16[2,1024,4096]{2,1,0:T(8,128)(2,1)S(1)} %bitcast.60, f32[1024,128]{0,1:T(8,128)S(1)} %get-tuple-element.8, bf16[128,4096]{1,0:T(8,128)(2,1)S(1)} %copy-done.2), kind=kOutput, calls=%fused_computation.36 | convolution fusion | flops 539492352 | bytes 6029312 | tf_op jit(solution)/shard_map/dot_general | solution.py:29
  137.2 3.8 %convolution_convert_fusion = bf16[1024,1024]{1,0:T(8,128)(2,1)} fusion(bf16[1024,256]{0,1:T(8,128)(2,1)S(1)} %collective-permute-done.5, bf16[1024,128]{0,1:T(8,128)(2,1)S(1)} %collective-permute-done.4, bf16[1024,128]{0,1:T(8,128)(2,1)S(1)} %get-tuple-element.7, bf16[128,1024]{1,0:T(8,128)(2,1)} %collective-permute-done.8, ...), kind=kOutput, calls=%fused_computation.32 | convolution fusion | flops 1082130432 | bytes 4194304 | tf_op jit(solution)/shard_map/dot_general | solution.py:25
  141.0 6.9 %all-to-all-start = ((bf16[32,32,1024]{2,1,0:T(8,128)(2,1)}), bf16[32,32,1024]{2,1,0:T(8,128)(2,1)S(1)}, u32[]{:S(2)}, u32[]{:S(2)}) async-start(bf16[32,32,1024]{2,1,0:T(8,128)(2,1)} %bitcast.53), calls=%async_computation | async-start | bytes 4194304 | tf_op jit(solution)/shard_map/all_to_all | solution.py:105
  147.9 2.9 %fusion.9 = bf16[128,2048]{1,0:T(8,128)(2,1)S(1)} fusion(bf16[1024,128]{0,1:T(8,128)(2,1)S(1)} %copy-done.6, bf16[2,1024,4096]{2,1,0:T(8,128)(2,1)} %bitcast.56), kind=kOutput, calls=%fused_computation.18 | convolution fusion | flops 537133056 | bytes 4980736 | tf_op jit(solution)/shard_map/dot_general | solution.py:29
  150.9 3.5 %fusion.10 = bf16[2048,128]{1,0:T(8,128)(2,1)S(1)} fusion(bf16[1024,128]{0,1:T(8,128)(2,1)S(1)} %copy-done.9, bf16[2,1024,4096]{2,1,0:T(8,128)(2,1)} %bitcast.57), kind=kOutput, calls=%fused_computation.19 | convolution fusion | flops 537133056 | bytes 4980736 | tf_op jit(solution)/shard_map/dot_general | solution.py:29
  154.4 3.6 %fusion.11 = bf16[2048,128]{1,0:T(8,128)(2,1)S(1)} fusion(bf16[1024,128]{0,1:T(8,128)(2,1)S(1)} %copy-done.9, bf16[2,1024,4096]{2,1,0:T(8,128)(2,1)} %bitcast.58), kind=kOutput, calls=%fused_computation.20 | convolution fusion | flops 537133056 | bytes 4980736 | tf_op jit(solution)/shard_map/dot_general | solution.py:29
  160.1 16.3 %all-to-all-done = bf16[32,32,1024]{2,1,0:T(8,128)(2,1)S(1)} async-done(((bf16[32,32,1024]{2,1,0:T(8,128)(2,1)}), bf16[32,32,1024]{2,1,0:T(8,128)(2,1)S(1)}, u32[]{:S(2)}, u32[]{:S(2)}) %all-to-all-start) | async-done | bytes 2097184 | tf_op jit(solution)/shard_map/all_to_all | solution.py:105
  176.7 3.1 %scatter_custom_fusion = f32[256,1024]{1,0:T(8,128)} fusion(f32[256,1024]{1,0:T(8,128)} %convert_add_fusion, s32[32]{0:T(128)S(1)} %fusion.58, f32[32,1024]{1,0:T(8,128)S(1)} %convert_reduce_fusion, f32[32]{0:T(128)S(1)} %compare_select_fusion.1), kind=kCustom, calls=%fused_computation.74 | custom fusion | flops 65536 | bytes 1180160 | tf_op jit(solution)/shard_map/scatter-add | solution.py:108
  179.8 2.1 %convert_element_type.40 = bf16[256,1024]{1,0:T(8,128)(2,1)} convert(f32[256,1024]{1,0:T(8,128)} %scatter_custom_fusion) | non-fusion elementwise | flops 262144 | bytes 1572864 | tf_op jit(solution)/shard_map/convert_element_type | solution.py:108
  (51 shorter events, 15.9 us)
Async XLA Ops:
  7.2 2.3 %copy-start = (bf16[256,2048]{1,0:T(8,128)(2,1)S(1)}, bf16[256,2048]{1,0:T(8,128)(2,1)}, u32[]{:S(2)}) copy-start(bf16[256,2048]{1,0:T(8,128)(2,1)} %param.17) | copy-start | bytes 3145732
  7.2 24.1 %copy-start.3 = (bf16[256,2048]{1,0:T(8,128)(2,1)S(1)}, bf16[256,2048]{1,0:T(8,128)(2,1)}, u32[]{:S(2)}) copy-start(bf16[256,2048]{1,0:T(8,128)(2,1)} %param.9) | copy-start | bytes 3145732
  7.2 107.0 %all-gather.2.cloned.1.call-start = ((), (), s32[]{:S(2)}) async-start(), calls=%async_computation.1 | async-start | bytes 16908288 | tf_op jit(solution)/shard_map/all_gather | solution.py:70
  14.0 15.1 %collective-permute-start = (bf16[128,2048]{1,0:T(8,128)(2,1)S(1)}, bf16[128,2048]{1,0:T(8,128)(2,1)S(1)}, u32[]{:S(2)}, u32[]{:S(2)}) collective-permute-start(bf16[128,2048]{1,0:T(8,128)(2,1)S(1)} %constant_dynamic-slice_fusion.5), channel_id=1, source_target_pairs={{0,1},{1,0},{2,3},{3,2},{4,5},{5,4},{6,7},{7,6},{8,9},{9,8},{10,11... | collective-permute-start | bytes 1572872 | tf_op jit(solution)/shard_map/ppermute | solution.py:86
  29.1 1.9 %collective-permute-start.1 = (bf16[128,2048]{1,0:T(8,128)(2,1)S(1)}, bf16[128,2048]{1,0:T(8,128)(2,1)S(1)}, u32[]{:S(2)}, u32[]{:S(2)}) collective-permute-start(bf16[128,2048]{1,0:T(8,128)(2,1)S(1)} %collective-permute-done), channel_id=1, source_target_pairs={{0,64},{64,0},{1,65},{65,1},{2,66},{66,2},{3,67},{67,3},{4,68},{68... | collective-permute-start | bytes 1572872 | tf_op jit(solution)/shard_map/ppermute | solution.py:87
  31.3 3.8 %copy-start.1 = (bf16[512,4096]{1,0:T(8,128)(2,1)S(1)}, bf16[512,4096]{1,0:T(8,128)(2,1)}, u32[]{:S(2)}) copy-start(bf16[512,4096]{1,0:T(8,128)(2,1)} %param.11) | copy-start | bytes 12582916
  35.8 4.4 %collective-permute-start.2 = (f32[256,2048]{1,0:T(8,128)S(1)}, f32[256,2048]{1,0:T(8,128)}, u32[]{:S(2)}, u32[]{:S(2)}) collective-permute-start(f32[256,2048]{1,0:T(8,128)S(1)} %fusion.18), channel_id=1, source_target_pairs={{0,64},{64,0},{1,65},{65,1},{2,66},{66,2},{3,67},{67,3},{4,68},{68... | collective-permute-start | bytes 6291464 | tf_op jit(solution)/shard_map/ppermute | solution.py:92
  36.0 17.4 %copy-start.8 = (s32[1,32]{1,0:T(1,128)S(1)}, s32[1,32]{1,0:T(1,128)}, u32[]{:S(2)}) copy-start(s32[1,32]{1,0:T(1,128)} %param.14) | copy-start | bytes 388
  44.0 22.3 %collective-permute-start.3 = (bf16[256,1024]{1,0:T(8,128)(2,1)}, bf16[256,1024]{1,0:T(8,128)(2,1)}, u32[]{:S(2)}, u32[]{:S(2)}) collective-permute-start(bf16[256,1024]{1,0:T(8,128)(2,1)} %dynamic-slice_convert_fusion), channel_id=1, source_target_pairs={{0,1},{1,0},{2,3},{3,2},{4,5},{5,4},{6,7},{7,6},{8,9},{9,8},{10,11... | collective-permute-start | bytes 1572872 | tf_op jit(solution)/shard_map/ppermute | solution.py:93
  49.8 87.3 %collective-permute-start.8 = (bf16[128,1024]{1,0:T(8,128)(2,1)}, bf16[128,1024]{1,0:T(8,128)(2,1)}, u32[]{:S(2)}, u32[]{:S(2)}) collective-permute-start(bf16[128,1024]{1,0:T(8,128)(2,1)} %get-tuple-element.4), channel_id=1, source_target_pairs={{0,65},{1,64},{64,1},{65,0},{2,67},{3,66},{66,3},{67,2},{4,69},{5,... | collective-permute-start | bytes 786440 | tf_op jit(solution)/shard_map/ppermute | solution.py:81
  49.8 87.3 %collective-permute-start.7 = (bf16[128,1024]{1,0:T(8,128)(2,1)}, bf16[128,1024]{1,0:T(8,128)(2,1)}, u32[]{:S(2)}, u32[]{:S(2)}) collective-permute-start(bf16[128,1024]{1,0:T(8,128)(2,1)} %get-tuple-element.5), channel_id=1, source_target_pairs={{0,64},{1,65},{64,0},{65,1},{2,66},{3,67},{66,2},{67,3},{4,68},{5,... | collective-permute-start | bytes 786440 | tf_op jit(solution)/shard_map/ppermute | solution.py:81
  49.9 87.2 %collective-permute-start.6 = (bf16[128,1024]{1,0:T(8,128)(2,1)}, bf16[128,1024]{1,0:T(8,128)(2,1)}, u32[]{:S(2)}, u32[]{:S(2)}) collective-permute-start(bf16[128,1024]{1,0:T(8,128)(2,1)} %get-tuple-element.6), channel_id=1, source_target_pairs={{0,1},{1,0},{64,65},{65,64},{2,3},{3,2},{66,67},{67,66},{4,5},{5,4... | collective-permute-start | bytes 786440 | tf_op jit(solution)/shard_map/ppermute | solution.py:81
  114.2 11.8 %copy-start.7 = (bf16[2048,4096]{1,0:T(8,128)(2,1)S(1)}, bf16[2048,4096]{1,0:T(8,128)(2,1)}, u32[]{:S(2)}) copy-start(bf16[2048,4096]{1,0:T(8,128)(2,1)} %all-gather.2.cloned.1.call-done) | copy-start | bytes 50331652
  118.2 7.8 %copy-start.2 = (bf16[128,4096]{1,0:T(8,128)(2,1)S(1)}, bf16[128,4096]{1,0:T(8,128)(2,1)}, u32[]{:S(2)}) copy-start(bf16[128,4096]{1,0:T(8,128)(2,1)} %param.13) | copy-start | bytes 3145732
  122.9 14.3 %copy-start.5 = (bf16[1024,128]{0,1:T(8,128)(2,1)}, bf16[1024,128]{0,1:T(8,128)(2,1)S(1)}, u32[]{:S(2)}) copy-start(bf16[1024,128]{0,1:T(8,128)(2,1)S(1)} %get-tuple-element.7) | copy-start | bytes 786436
  122.9 10.0 %collective-permute-start.4 = (bf16[1024,128]{0,1:T(8,128)(2,1)S(1)}, bf16[1024,128]{0,1:T(8,128)(2,1)S(1)}, u32[]{:S(2)}, u32[]{:S(2)}) collective-permute-start(bf16[1024,128]{0,1:T(8,128)(2,1)S(1)} %get-tuple-element.7), channel_id=1, source_target_pairs={{0,1},{1,0},{2,3},{3,2},{4,5},{5,4},{6,7},{7,6},{8,9},{9,8},{10,11... | collective-permute-start | bytes 786440 | tf_op jit(solution)/shard_map/ppermute | solution.py:101
  133.0 4.2 %collective-permute-start.5 = (bf16[1024,256]{0,1:T(8,128)(2,1)S(1)}, bf16[1024,256]{0,1:T(8,128)(2,1)S(1)}, u32[]{:S(2)}, u32[]{:S(2)}) collective-permute-start(bf16[1024,256]{0,1:T(8,128)(2,1)S(1)} %pad_maximum_fusion.2), channel_id=1, source_target_pairs={{0,64},{64,0},{1,65},{65,1},{2,66},{66,2},{3,67},{67,3},{4,68},{68... | collective-permute-start | bytes 1572872 | tf_op jit(solution)/shard_map/ppermute | solution.py:103
  141.0 6.9 %copy-start.6 = (bf16[1024,128]{0,1:T(8,128)(2,1)S(1)}, bf16[1024,128]{0,1:T(8,128)(2,1)}, u32[]{:S(2)}) copy-start(bf16[1024,128]{0,1:T(8,128)(2,1)} %copy-done.5) | copy-start | bytes 786436
  141.0 35.4 %all-to-all-start = ((bf16[32,32,1024]{2,1,0:T(8,128)(2,1)}), bf16[32,32,1024]{2,1,0:T(8,128)(2,1)S(1)}, u32[]{:S(2)}, u32[]{:S(2)}) async-start(bf16[32,32,1024]{2,1,0:T(8,128)(2,1)} %bitcast.53), calls=%async_computation | async-start | bytes 4194304 | tf_op jit(solution)/shard_map/all_to_all | solution.py:105
  147.9 3.0 %copy-start.9 = (bf16[1024,128]{0,1:T(8,128)(2,1)S(1)}, bf16[1024,128]{0,1:T(8,128)(2,1)}, u32[]{:S(2)}) copy-start(bf16[1024,128]{0,1:T(8,128)(2,1)} %fusion.25) | copy-start | bytes 786436
  154.4 4.6 %copy-start.4 = (bf16[128,2048]{1,0:T(8,128)(2,1)S(1)}, bf16[128,2048]{1,0:T(8,128)(2,1)}, u32[]{:S(2)}) copy-start(bf16[128,2048]{1,0:T(8,128)(2,1)} %fusion.8) | copy-start | bytes 1572868
Sparse Core Ops, SparseCore 0:
  13.0 101.1 all-gather.1
